TPU v7x, 32 devices: a whole 2x2x4 slice. The times are simulated.
32 devices in a mesh: tab: 2 (over x), cand: 4 (over z), dp: 4 (over y, core).
Axes of the slice: x: 2, y: 2, z: 4, core: 2. Of those that a mesh axis runs over, the one named last changes fastest.
Arguments:
- tables: bfloat16 [16, 65536, 128], P(('cand', 'dp'), 'tab'), may hold values from -6 to 6
- bag_ids: int32 [16, 1024, 16], P(('cand', 'dp')), may hold values from 0 to 65535
- bag_lengths: int32 [16, 1024], P(('cand', 'dp')), may hold values from 1 to 16
- item_weight: bfloat16 [2048, 256], replicated, may hold values from -0.125 to 0.125
- user_features: bfloat16 [16384, 512], P(('tab', 'dp')), may hold values from -6 to 6
- user_w1: bfloat16 [512, 1024], replicated, may hold values from -0.25 to 0.25
- user_w2: bfloat16 [1024, 256], replicated, may hold values from -0.1875 to 0.1875
- positive_items: int32 [16384], P(('tab', 'dp')), may hold values from 0 to 1023
Outputs:
- item_emb: float32 [1024, 256], P(('tab', 'cand', 'dp'))
- user_loss: float32 [16384], P(('tab', 'dp'))
Inputs may be any that keep to these rules, and one draw needn't show every extreme that they name: `bag_ids`: row ids of a table. Only the first bag_lengths ids of a bag count; the rest is padding.
All inputs are finite; a program needn't handle non-finite values.
Results may differ from a plain program's by a relative error of at most 0.00046.
Values sent between devices are 32-bit elements; how exact they have to be, the bound alone decides.
No kernel may reach another device: no remote copies, remote signals or barrier semaphores. Data moves between devices by JAX's collectives and lax.ppermute only.
A program may use at most 64 MiB of HBM per device.

v0:
```python
import functools

import jax
import jax.numpy as jnp
from jax import lax
from jax.experimental import pallas as pl
from jax.experimental.pallas import tpu as pltpu
from jax.sharding import PartitionSpec as P


epsilon = 1e-06
logit_scale = 20.0
log2_e = 1.4426950408889634
ln_2 = 0.6931471805599453


f32 = jnp.float32
bf16 = jnp.bfloat16
VMEM = pl.BlockSpec(memory_space=pltpu.VMEM)
SMEM = pl.BlockSpec(memory_space=pltpu.SMEM)
ANY = pl.BlockSpec(memory_space=pl.ANY)
MIB = 1 << 20
zero_rows = 8
bags_at_once = 8
tower_parts = 4


def widen_kernel(pieces, table_ref, wide_ref, raw, sems):
    rows = table_ref.shape[0]
    piece = rows // pieces
    block = min(256, piece)
    copies = [
        pltpu.make_async_copy(
            table_ref.at[pl.ds(k * piece, piece)], raw.at[pl.ds(k * piece, piece)], sems.at[k]
        )
        for k in range(pieces)
    ]
    for copy in copies:
        copy.start()
    wide_ref[pl.ds(rows, zero_rows), :] = jnp.zeros((zero_rows, wide_ref.shape[1]), f32)
    for k in range(pieces):
        copies[k].wait()

        @pl.loop(0, piece // block)
        def _(i):
            at = pl.ds(pl.multiple_of(k * piece + i * block, block), block)
            wide_ref[at, :] = raw[at, :].astype(f32)


def widen(table):
    rows, width = table.shape
    pieces = 16
    return pl.pallas_call(
        functools.partial(widen_kernel, pieces),
        out_shape=pltpu.VMEM((rows + zero_rows, width), f32),
        in_specs=[pl.BlockSpec(memory_space=pltpu.HBM)],
        out_specs=VMEM,
        scratch_shapes=[pltpu.VMEM((rows, width), bf16), pltpu.SemaphoreType.DMA((pieces,))],
        compiler_params=pltpu.CompilerParams(vmem_limit_bytes=30 * MIB),
        cost_estimate=pl.CostEstimate(flops=10**6, bytes_accessed=rows * width * 2, transcendentals=0),
        name="widen",
    )(table)


def place_kernel(T, C, rows, ids_ref, lengths_ref, after_ref, places_ref, inverse_ref):
    positions, items = ids_ref.shape
    run = items // (T * C)
    local = ids_ref[...] - lax.axis_index("tab") * rows
    valid = lax.broadcasted_iota(jnp.int32, local.shape, 0) < lengths_ref[...]
    places = jnp.where((local >= 0) & (local < rows) & valid, local, rows)
    inverse = 1.0 / lengths_ref[...].astype(f32)
    for t in range(T):
        for c in range(C):
            at = (t * C + c) * run
            to = pl.ds(c * positions * T + t, positions, stride=T)
            places_ref[to, :] = places[:, at : at + run]
            inverse_ref[pl.ds(c * T + t, 1), :] = inverse[:, at : at + run]


def place(ids, lengths, wide, T, C):
    positions, items = ids.shape
    rows = wide.shape[0] - zero_rows
    run = items // (T * C)
    if run % 128 == 0:
        places, inverse = pl.pallas_call(
            functools.partial(place_kernel, T, C, rows),
            out_shape=(
                jax.ShapeDtypeStruct((C * positions * T, run), jnp.int32),
                jax.ShapeDtypeStruct((C * T, run), f32),
            ),
            in_specs=[VMEM, VMEM, ANY],
            out_specs=(VMEM, VMEM),
            compiler_params=pltpu.CompilerParams(vmem_limit_bytes=4 * MIB),
            name="place",
        )(ids, lengths, wide)
        return places.reshape(-1), inverse.reshape(-1)
    local = ids - lax.axis_index("tab") * rows
    valid = lax.broadcasted_iota(jnp.int32, ids.shape, 0) < lengths
    places = jnp.where((local >= 0) & (local < rows) & valid, local, rows)
    places = places.reshape(positions, T, C, run).transpose(2, 0, 1, 3).reshape(-1)
    inverse = (1.0 / lengths.astype(f32)).reshape(T, C, run).transpose(1, 0, 2).reshape(-1)
    return places, inverse


def pool_kernel(positions, aheads, inverse_ref, wide_ref, places_ref, after_ref, *refs):
    count = refs[0].shape[0]
    out_refs = refs[: len(aheads)]
    places, inverse, sems = refs[len(aheads) :]
    size = count * positions
    chunks = [lax.rem(lax.axis_index("cand") + j, lax.axis_size("cand")) for j in aheads]
    copies = [pltpu.make_async_copy(inverse_ref, inverse, sems.at[0])]
    for k, chunk in enumerate(chunks):
        start = pl.multiple_of(chunk * size, size)
        copies.append(
            pltpu.make_async_copy(
                places_ref.at[pl.ds(start, size)], places.at[pl.ds(k * size, size)], sems.at[k + 1]
            )
        )
    for copy in copies:
        copy.start()
    copies[0].wait()
    for k, chunk in enumerate(chunks):
        copies[k + 1].wait()
        out_ref = out_refs[k]

        @pl.loop(0, count // bags_at_once)
        def _(b):
            for u in range(bags_at_once):
                i = b * bags_at_once + u
                rows = [
                    wide_ref[pl.ds(places.at[pl.ds(k * size + p * count, count)][i], 1), :]
                    for p in range(positions)
                ]
                while len(rows) > 1:
                    rows = [sum(rows[n : n + 2][1:], rows[n]) for n in range(0, len(rows), 2)]
                out_ref[pl.ds(i, 1), :] = rows[0] * inverse[chunk * count + i]


def pool(aheads, inverse, wide, places, after, count, positions):
    width = wide.shape[1]
    return pl.pallas_call(
        functools.partial(pool_kernel, positions, aheads),
        out_shape=(jax.ShapeDtypeStruct((count, width), f32),) * len(aheads),
        in_specs=[ANY, VMEM, ANY, ANY],
        out_specs=(VMEM,) * len(aheads),
        scratch_shapes=[
            pltpu.SMEM((len(aheads) * count * positions,), jnp.int32),
            pltpu.SMEM(inverse.shape, f32),
            pltpu.SemaphoreType.DMA((len(aheads) + 1,)),
        ],
        compiler_params=pltpu.CompilerParams(vmem_limit_bytes=20 * MIB),
        cost_estimate=pl.CostEstimate(
            flops=10**7 * len(aheads), bytes_accessed=count * width * 4, transcendentals=0
        ),
        name="pool",
    )(inverse, wide, places, after)


def project_kernel(order, *refs):
    count = len(order)
    parts, weight_ref, send_ref, keep_ref = refs[:count], refs[count], refs[-2], refs[-1]
    half = send_ref.shape[0]
    width = parts[0].shape[1]
    c, d = lax.axis_index("cand"), lax.axis_index("dp")
    C, D = lax.axis_size("cand"), lax.axis_size("dp")
    own_half = lax.rem(d, 2)
    for which, out_ref in ((1 - own_half, send_ref), (own_half, keep_ref)):
        at = pl.ds(pl.multiple_of(which * half, half), half)
        total = None
        for k in range(count):
            value = parts[k][at, :]
            source = lax.rem(c + C - order[k], C) * D + d
            weight = weight_ref[pl.ds(pl.multiple_of(source * width, width), width), :]
            for _ in range(3):
                short = value.astype(bf16)
                term = jnp.dot(short, weight, preferred_element_type=f32)
                total = term if total is None else total + term
                value = value - short.astype(f32)
        out_ref[...] = total


def project(order, parts, weight):
    rows = parts[0].shape[0]
    shape = jax.ShapeDtypeStruct((rows // 2, weight.shape[1]), f32)
    return pl.pallas_call(
        functools.partial(project_kernel, order),
        out_shape=(shape, shape),
        in_specs=[VMEM] * (len(parts) + 1),
        out_specs=(VMEM, VMEM),
        compiler_params=pltpu.CompilerParams(vmem_limit_bytes=8 * MIB),
        cost_estimate=pl.CostEstimate(flops=10**8, bytes_accessed=2 * MIB, transcendentals=0),
        name="project",
    )(*parts, weight)


def tower_kernel(block, features_ref, w1_ref, w2_ref, after_ref, high_ref, low_ref):
    for start in range(0, features_ref.shape[0], block):
        at = pl.ds(start, block)
        hidden = jnp.dot(features_ref[at, :], w1_ref[...], preferred_element_type=f32)
        hidden = 0.5 * hidden * (1.0 + lax.erf(hidden * (0.5**0.5)))
        emb = jnp.dot(hidden.astype(bf16), w2_ref[...], preferred_element_type=f32)
        emb = emb * lax.rsqrt(jnp.mean(emb * emb, axis=1, keepdims=True) + epsilon)
        high = emb.astype(bf16)
        high_ref[at, :] = high
        low_ref[at, :] = (emb - high.astype(f32)).astype(bf16)


def tower(part, parts, features, w1, w2, after):
    users = features.shape[0] // parts
    embed = w2.shape[1]
    whole = lambda i: (0, 0)
    shape = jax.ShapeDtypeStruct((users, embed), bf16)
    return pl.pallas_call(
        functools.partial(tower_kernel, min(256, users)),
        grid=(1,),
        out_shape=(shape, shape),
        in_specs=[
            pl.BlockSpec((users, features.shape[1]), lambda i: (part, 0)),
            VMEM,
            VMEM,
            ANY,
        ],
        out_specs=(pl.BlockSpec((users, embed), whole), pl.BlockSpec((users, embed), whole)),
        compiler_params=pltpu.CompilerParams(vmem_limit_bytes=16 * MIB),
        cost_estimate=pl.CostEstimate(
            flops=2 * users * (w1.size + w2.size), bytes_accessed=2 * MIB, transcendentals=users * w1.shape[1]
        ),
    )(features, w1, w2, after)


def split(x, size):
    if size & (size - 1) == 0:
        return x >> (size.bit_length() - 1), x & (size - 1)
    return lax.div(x, jnp.full_like(x, size)), lax.rem(x, jnp.full_like(x, size))


def scores_kernel(count, block, own, positive_ref, mine_ref, other_ref, *refs):
    item_ref, out_ref = refs[-2:]
    t, c, d = (lax.axis_index(axis) for axis in ("tab", "cand", "dp"))
    C, D = lax.axis_size("cand"), lax.axis_size("dp")
    half = mine_ref.shape[0]
    first = lax.rem(d, 2) * half
    items = jnp.concatenate([mine_ref[...], other_ref[...]], axis=0)
    items = items * (logit_scale / items.shape[1] * log2_e)
    item_high = items.astype(bf16)
    item_low = (items - item_high.astype(f32)).astype(bf16)
    users = refs[0].shape[0]

    def dot(a, b):
        return lax.dot_general(a, b, (((1,), (1,)), ((), ())), preferred_element_type=f32)

    for k in range(count):
        high_ref, low_ref = refs[2 * k], refs[2 * k + 1]
        for start in range(0, users, block):
            at = pl.ds(start, block)
            high = high_ref[at, :]
            scores = dot(item_high, high) + (dot(item_low, high) + dot(item_high, low_ref[at, :]))
            to = pl.ds(k * users + start, block)
            rest, within = split(positive_ref[:, to], own)
            rest, owner_d = split(rest, D)
            owner_t, owner_c = split(rest, C)
            place = (owner_t * D + owner_d) * own + within - first
            place = jnp.where(place < 0, place + 2 * half, place)
            place = jnp.where(owner_c == c, place, -1)
            here = lax.broadcasted_iota(jnp.int32, scores.shape, 0) == place
            out_ref[pl.ds(0, 1), to] = jnp.sum(jnp.exp2(scores), axis=0, keepdims=True)
            out_ref[pl.ds(1, 1), to] = jnp.sum(
                jnp.where(here, scores, 0.0), axis=0, keepdims=True
            )
    row = (t * D + d) * own - first
    inside = (row >= 0) & (row < half)

    step = 8 if own % 8 == 0 else 1

    def copy_rows(from_ref, start):
        for k in range(0, own, step):
            at = pl.ds(pl.multiple_of(start + k, step), step)
            item_ref[pl.ds(k, step), :] = from_ref[at, :]

    @pl.when(inside)
    def _():
        copy_rows(mine_ref, row)

    @pl.when(jnp.logical_not(inside))
    def _():
        copy_rows(other_ref, lax.rem(row + 2 * half, half))


def score(positives, mine, other, embs, own):
    count = len(embs)
    users = embs[0][0].shape[0]
    flat = [x for pair in embs for x in pair]
    total = users * count
    return pl.pallas_call(
        functools.partial(scores_kernel, count, min(512, users), own),
        out_shape=(
            jax.ShapeDtypeStruct((own, mine.shape[1]), f32),
            jax.ShapeDtypeStruct((2, total), f32),
        ),
        in_specs=[VMEM] * (3 + len(flat)),
        out_specs=(VMEM, VMEM),
        compiler_params=pltpu.CompilerParams(vmem_limit_bytes=16 * MIB),
        cost_estimate=pl.CostEstimate(
            flops=6 * total * mine.shape[1] * 2 * mine.shape[0], bytes_accessed=2 * MIB, transcendentals=0
        ),
        name="score",
    )(positives, mine, other, *flat)


def swap(x, axis, bit):
    return lax.ppermute(x, axis, [(i, i ^ bit) for i in range(lax.axis_size(axis))])


def swap_both(x, bit_dp, bit_tab):
    T, D = lax.axis_size("tab"), lax.axis_size("dp")
    pairs = [(t * D + d, (t ^ bit_tab) * D + (d ^ bit_dp)) for t in range(T) for d in range(D)]
    return lax.ppermute(x, ("tab", "dp"), pairs)


def shift(x, axis, by):
    size = lax.axis_size(axis)
    return lax.ppermute(x, axis, [(i, (i + by) % size) for i in range(size)])


def bits_of(axis):
    return [(axis, 1 << k) for k in range(lax.axis_size(axis).bit_length() - 1)]


def body(
    tables, bag_ids, bag_lengths, item_weight, user_features, user_w1, user_w2, positive_items
):
    table = tables[0]
    ids = bag_ids[0].T
    T, C, D = lax.axis_size("tab"), lax.axis_size("cand"), lax.axis_size("dp")
    positions, items = ids.shape
    own = items // (T * C * D)
    count = items // C

    wide = widen(table)
    places, inverse = place(ids, bag_lengths, wide, T, C)
    groups = pool_groups(C)
    order = sum(groups, ())
    after = places
    received = []
    for group in groups:
        parts = pool(group, inverse, wide, places, after, count, positions)
        after = parts[-1]
        for j, part in zip(group, parts):
            if j:
                part = shift(part, "cand", j)
            received.append(part)

    send, keep = project(order, received, item_weight)
    total = keep + swap(send, "dp", 1)
    embs = []
    for k in range(tower_parts):
        embs.append(tower(k, tower_parts, user_features, user_w1, user_w2, keep))
    steps = [step for step in bits_of("dp") if step[1] > 1] + bits_of("tab")
    if len(steps) == 2:
        moved = []
        for picked in ((1, 1), (1, 0), (0, 1)):
            moved.append(swap_both(total, picked[0] * steps[0][1], picked[1] * steps[1][1]))
        total = (total + moved[1]) + (moved[2] + moved[0])
    else:
        for step in steps:
            total = total + swap(total, *step)
    mine = total * lax.rsqrt(jnp.mean(total * total, axis=1, keepdims=True) + epsilon)
    other = swap(mine, "dp", 1)
    item_emb, partial = score(positive_items[None], mine, other, embs, own)
    summed = partial
    for j in range(1, C):
        summed = summed + swap(partial, "cand", j)
    user_loss = (jnp.log2(summed[0]) - summed[1]) * ln_2
    return (item_emb, user_loss)


def pool_groups(C):
    order = sorted(range(1, C), key=lambda j: -min(j, C - j))
    return tuple(group for group in ((order[0],), tuple(order[1:]), (0,)) if group)


def solution(mesh):
    placed = (
        P(("cand", "dp"), "tab", None),
        P(("cand", "dp"), None, None),
        P(("cand", "dp"), None),
        P(),
        P(("tab", "dp"), None),
        P(),
        P(),
        P(("tab", "dp")),
    )
    return jax.shard_map(
        body,
        mesh=mesh,
        in_specs=placed,
        out_specs=(P(("tab", "cand", "dp"), None), P(("tab", "dp"))),
        check_vma=False,
    )
```

profile of v0, /device:TPU:0, one launch (start us, length us, event | category | flops | bytes accessed | tf_op | source)
XLA Modules:
  0.0 51.7 jit_solution(6437421132667393576)
XLA Ops:
  0.6 0.0 copy-start.4
  0.6 0.0 copy-start.5
  0.6 3.6 %widen.1.after_ref.wide_ref = f32[32776,128]{1,0:T(8,128)S(1)} custom-call(bf16[32768,128]{1,0:T(8,128)(2,1)} %bitcast.17), custom_call_target="tpu_custom_call" | custom-call | flops 1000000 | bytes 8388608 | tf_op jit(solution)/shard_map/widen/pallas_call | solution.py:53
  4.3 0.0 copy-done.4
  4.3 0.0 copy-done.5
  4.3 3.9 %pool.3.after_ref = f32[256,128]{1,0:T(8,128)S(1)} custom-call(f32[1024]{0:T(1024)S(1)} %bitcast.13, f32[32776,128]{1,0:T(8,128)S(1)} %widen.1.after_ref.wide_ref, s32[16384]{0:T(1024)S(1)} %bitcast.8, s32[16384]{0:T(1024)S(1)} %bitcast.9), custom_call_target="tpu_custom_call" | custom-call | flops 10000000 | bytes 131072 | tf_op jit(solution)/shard_map/pool/pallas_call | solution.py:141
  8.2 4.1 %collective-permute-start = (f32[256,128]{1,0:T(8,128)S(1)}, f32[256,128]{1,0:T(8,128)S(1)}, u32[]{:S(2)}, u32[]{:S(2)}) collective-permute-start(f32[256,128]{1,0:T(8,128)S(1)} %pool.3.after_ref), channel_id=1, source_target_pairs={{0,8},{4,12},{8,0},{12,4},{1,9},{5,13},{9,1},{13,5},{2,10},{6,14},... | collective-permute-start | bytes 393224 | tf_op jit(solution)/shard_map/ppermute | solution.py:322
  12.3 6.9 %pool.4 = (f32[256,128]{1,0:T(8,128)S(1)}, f32[256,128]{1,0:T(8,128)S(1)}) custom-call(f32[1024]{0:T(1024)S(1)} %bitcast.14, f32[32776,128]{1,0:T(8,128)S(1)} %widen.1.after_ref.wide_ref, s32[16384]{0:T(1024)S(1)} %bitcast.10, f32[256,128]{1,0:T(8,128)S(1)} %pool.3.after_ref), custom_call_target="tpu_custom_call" | custom-call | flops 20000000 | bytes 131072 | tf_op jit(solution)/shard_map/pool/pallas_call | solution.py:141
  19.2 1.6 %collective-permute-start.1 = (f32[256,128]{1,0:T(8,128)S(1)}, f32[256,128]{1,0:T(8,128)S(1)}, u32[]{:S(2)}, u32[]{:S(2)}) collective-permute-start(f32[256,128]{1,0:T(8,128)S(1)} %get-tuple-element.20), channel_id=1, source_target_pairs={{0,4},{4,8},{8,12},{12,0},{1,5},{5,9},{9,13},{13,1},{2,6},{6,10},{... | collective-permute-start | bytes 393224 | tf_op jit(solution)/shard_map/ppermute | solution.py:322
  20.8 0.0 copy-start.3
  20.8 0.0 copy-start
  20.8 0.0 copy-start.1
  20.8 0.0 copy-start.2
  20.9 2.3 %collective-permute-start.2 = (f32[256,128]{1,0:T(8,128)S(1)}, f32[256,128]{1,0:T(8,128)S(1)}, u32[]{:S(2)}, u32[]{:S(2)}) collective-permute-start(f32[256,128]{1,0:T(8,128)S(1)} %get-tuple-element.21.after_ref), channel_id=1, source_target_pairs={{0,12},{4,0},{8,4},{12,8},{1,13},{5,1},{9,5},{13,9},{2,14},{6,2},{... | collective-permute-start | bytes 393224 | tf_op jit(solution)/shard_map/ppermute | solution.py:322
  23.2 3.9 %pool.5.refs_3_ = f32[256,128]{1,0:T(8,128)S(1)} custom-call(f32[1024]{0:T(1024)S(1)} %bitcast.15, f32[32776,128]{1,0:T(8,128)S(1)} %widen.1.after_ref.wide_ref, s32[16384]{0:T(1024)S(1)} %bitcast.11, f32[256,128]{1,0:T(8,128)S(1)} %get-tuple-element.21.after_ref), custom_call_target="tpu_custom_call" | custom-call | flops 10000000 | bytes 131072 | tf_op jit(solution)/shard_map/pool/pallas_call | solution.py:141
  27.0 0.0 collective-permute-done.refs_0_
  27.0 0.4 collective-permute-done.1.refs_1_
  27.4 1.0 %collective-permute-done.2.refs_2_ = f32[256,128]{1,0:T(8,128)S(1)} collective-permute-done((f32[256,128]{1,0:T(8,128)S(1)}, f32[256,128]{1,0:T(8,128)S(1)}, u32[]{:S(2)}, u32[]{:S(2)}) %collective-permute-start.2) | collective-permute-done | bytes 131104 | tf_op jit(solution)/shard_map/ppermute | solution.py:322
  28.4 0.0 copy-done.3
  28.4 0.6 %project.1 = (f32[128,256]{1,0:T(8,128)S(1)}, f32[128,256]{1,0:T(8,128)S(1)}) custom-call(f32[256,128]{1,0:T(8,128)S(1)} %collective-permute-done.refs_0_, f32[256,128]{1,0:T(8,128)S(1)} %collective-permute-done.1.refs_1_, f32[256,128]{1,0:T(8,128)S(1)} %collective-permute-done.2.refs_2_, f32[256,128]{1,0:T(8,128)S(1)} %pool.5.refs_3_, ...), custom_call_target="tpu_custom_call" | custom-call | flops 100000000 | bytes 2097152 | tf_op jit(solution)/shard_map/project/pallas_call | solution.py:185
  29.0 0.0 copy-start.6
  29.0 0.1 collective-permute-start.3
  29.0 1.3 %collective-permute-done.3 = f32[128,256]{1,0:T(8,128)S(1)} collective-permute-done((f32[128,256]{1,0:T(8,128)S(1)}, f32[128,256]{1,0:T(8,128)S(1)}, u32[]{:S(2)}, u32[]{:S(2)}) %collective-permute-start.3) | collective-permute-done | bytes 131104 | tf_op jit(solution)/shard_map/ppermute | solution.py:311
  30.4 2.5 %collective-permute-start.6 = (f32[128,256]{1,0:T(8,128)S(1)}, f32[128,256]{1,0:T(8,128)S(1)}, u32[]{:S(2)}, u32[]{:S(2)}) collective-permute-start(f32[128,256]{1,0:T(8,128)S(1)} %add.32), channel_id=1, source_target_pairs={{0,18},{1,19},{2,16},{3,17},{16,2},{17,3},{18,0},{19,1},{4,22},{5,... | collective-permute-start | bytes 393224 | tf_op jit(solution)/shard_map/ppermute | solution.py:317
  32.9 0.5 %collective-permute-start.5 = (f32[128,256]{1,0:T(8,128)S(1)}, f32[128,256]{1,0:T(8,128)S(1)}, u32[]{:S(2)}, u32[]{:S(2)}) collective-permute-start(f32[128,256]{1,0:T(8,128)S(1)} %add.32), channel_id=1, source_target_pairs={{0,16},{1,17},{2,18},{3,19},{16,0},{17,1},{18,2},{19,3},{4,20},{5,... | collective-permute-start | bytes 393224 | tf_op jit(solution)/shard_map/ppermute | solution.py:317
  33.4 0.5 collective-permute-start.4
  34.0 0.0 copy-done
  34.0 0.0 copy-done.1
  34.0 0.0 copy-done.2
  34.0 1.2 %shard_map.98 = (bf16[512,256]{1,0:T(8,128)(2,1)S(1)}, bf16[512,256]{1,0:T(8,128)(2,1)S(1)}) custom-call(bf16[2048,512]{1,0:T(8,128)(2,1)S(1)} %copy-done, bf16[512,1024]{1,0:T(8,128)(2,1)S(1)} %copy-done.1, bf16[1024,256]{1,0:T(8,128)(2,1)S(1)} %copy-done.2, f32[128,256]{1,0:T(8,128)S(1)} %get-tuple-element.22.after_ref), custom_call_target="tpu_custom_call" | custom-call | flops 805306368 | bytes 2097152 | tf_op jit(solution)/shard_map/pallas_call | solution.py:213
  35.2 1.2 %shard_map.97 = (bf16[512,256]{1,0:T(8,128)(2,1)S(1)}, bf16[512,256]{1,0:T(8,128)(2,1)S(1)}) custom-call(bf16[2048,512]{1,0:T(8,128)(2,1)S(1)} %copy-done, bf16[512,1024]{1,0:T(8,128)(2,1)S(1)} %copy-done.1, bf16[1024,256]{1,0:T(8,128)(2,1)S(1)} %copy-done.2, f32[128,256]{1,0:T(8,128)S(1)} %get-tuple-element.22.after_ref), custom_call_target="tpu_custom_call" | custom-call | flops 805306368 | bytes 2097152 | tf_op jit(solution)/shard_map/pallas_call | solution.py:213
  36.5 1.3 %collective-permute-done.6 = f32[128,256]{1,0:T(8,128)S(1)} collective-permute-done((f32[128,256]{1,0:T(8,128)S(1)}, f32[128,256]{1,0:T(8,128)S(1)}, u32[]{:S(2)}, u32[]{:S(2)}) %collective-permute-start.6) | collective-permute-done | bytes 131104 | tf_op jit(solution)/shard_map/ppermute | solution.py:317
  37.7 2.0 %collective-permute-done.5 = f32[128,256]{1,0:T(8,128)S(1)} collective-permute-done((f32[128,256]{1,0:T(8,128)S(1)}, f32[128,256]{1,0:T(8,128)S(1)}, u32[]{:S(2)}, u32[]{:S(2)}) %collective-permute-start.5) | collective-permute-done | bytes 131104 | tf_op jit(solution)/shard_map/ppermute | solution.py:317
  39.8 0.0 collective-permute-done.4
  39.8 0.1 multiply_reduce_fusion
  39.9 0.1 broadcast_multiply_fusion.mine_ref
  40.0 0.1 collective-permute-start.7
  40.1 1.2 %shard_map.96 = (bf16[512,256]{1,0:T(8,128)(2,1)S(1)}, bf16[512,256]{1,0:T(8,128)(2,1)S(1)}) custom-call(bf16[2048,512]{1,0:T(8,128)(2,1)S(1)} %copy-done, bf16[512,1024]{1,0:T(8,128)(2,1)S(1)} %copy-done.1, bf16[1024,256]{1,0:T(8,128)(2,1)S(1)} %copy-done.2, f32[128,256]{1,0:T(8,128)S(1)} %get-tuple-element.22.after_ref), custom_call_target="tpu_custom_call" | custom-call | flops 805306368 | bytes 2097152 | tf_op jit(solution)/shard_map/pallas_call | solution.py:213
  41.3 1.2 %shard_map.95 = (bf16[512,256]{1,0:T(8,128)(2,1)S(1)}, bf16[512,256]{1,0:T(8,128)(2,1)S(1)}) custom-call(bf16[2048,512]{1,0:T(8,128)(2,1)S(1)} %copy-done, bf16[512,1024]{1,0:T(8,128)(2,1)S(1)} %copy-done.1, bf16[1024,256]{1,0:T(8,128)(2,1)S(1)} %copy-done.2, f32[128,256]{1,0:T(8,128)S(1)} %get-tuple-element.22.after_ref), custom_call_target="tpu_custom_call" | custom-call | flops 805306368 | bytes 2097152 | tf_op jit(solution)/shard_map/pallas_call | solution.py:213
  42.6 0.0 collective-permute-done.7.other_ref
  42.6 0.0 copy-done.6
  42.6 1.8 %score.1 = (f32[32,256]{1,0:T(8,128)}, f32[2,2048]{1,0:T(2,128)S(1)}) custom-call(s32[1,2048]{1,0:T(1,128)S(1)} %bitcast.16, f32[128,256]{1,0:T(8,128)S(1)} %broadcast_multiply_fusion.mine_ref, f32[128,256]{1,0:T(8,128)S(1)} %collective-permute-done.7.other_ref, bf16[512,256]{1,0:T(8,128)(2,1)S(1)} %get-tuple-element.24.refs_0_, ...), custom_call_target="tpu_custom_call" | custom-call | flops 805306368 | bytes 2097152 | tf_op jit(solution)/shard_map/score/pallas_call | solution.py:294
  44.4 2.0 %collective-permute-start.10 = (f32[2,2048]{1,0:T(2,128)S(1)}, f32[2,2048]{1,0:T(2,128)S(1)}, u32[]{:S(2)}, u32[]{:S(2)}) collective-permute-start(f32[2,2048]{1,0:T(2,128)S(1)} %get-tuple-element.33), channel_id=1, source_target_pairs={{0,12},{4,8},{8,4},{12,0},{1,13},{5,9},{9,5},{13,1},{2,14},{6,10},... | collective-permute-start | bytes 49160 | tf_op jit(solution)/shard_map/ppermute | solution.py:311
  46.4 0.0 collective-permute-start.9
  46.4 2.4 %collective-permute-start.8 = (f32[2,2048]{1,0:T(2,128)S(1)}, f32[2,2048]{1,0:T(2,128)S(1)}, u32[]{:S(2)}, u32[]{:S(2)}) collective-permute-start(f32[2,2048]{1,0:T(2,128)S(1)} %get-tuple-element.33), channel_id=1, source_target_pairs={{0,4},{4,0},{8,12},{12,8},{1,5},{5,1},{9,13},{13,9},{2,6},{6,2},{1... | collective-permute-start | bytes 49160 | tf_op jit(solution)/shard_map/ppermute | solution.py:311
  48.8 1.1 %collective-permute-done.10 = f32[2,2048]{1,0:T(2,128)S(1)} collective-permute-done((f32[2,2048]{1,0:T(2,128)S(1)}, f32[2,2048]{1,0:T(2,128)S(1)}, u32[]{:S(2)}, u32[]{:S(2)}) %collective-permute-start.10) | collective-permute-done | bytes 16416 | tf_op jit(solution)/shard_map/ppermute | solution.py:311
  50.0 1.1 %collective-permute-done.9 = f32[2,2048]{1,0:T(2,128)S(1)} collective-permute-done((f32[2,2048]{1,0:T(2,128)S(1)}, f32[2,2048]{1,0:T(2,128)S(1)}, u32[]{:S(2)}, u32[]{:S(2)}) %collective-permute-start.9) | collective-permute-done | bytes 16416 | tf_op jit(solution)/shard_map/ppermute | solution.py:311
  51.1 0.0 collective-permute-done.8
  51.1 0.6 %fusion = f32[1,2048]{1,0:T(1,128)} fusion(f32[2,2048]{1,0:T(2,128)S(1)} %add_add_fusion.1), kind=kLoop, calls=%fused_computation.5 | loop fusion | flops 6144 | bytes 24576 | tf_op jit(solution)/shard_map/mul | solution.py:373
  (4 shorter events, 0.1 us)
Async XLA Ops:
  0.6 3.7 %copy-start.4 = (s32[1,1024,16]{1,2,0:T(8,128)S(1)}, s32[1,1024,16]{1,2,0:T(8,128)}, u32[]{:S(2)}) copy-start(s32[1,1024,16]{1,2,0:T(8,128)} %param.9) | copy-start | bytes 196612
  0.6 3.7 %copy-start.5 = (s32[1,1024]{1,0:T(1,128)S(1)}, s32[1,1024]{1,0:T(1,128)}, u32[]{:S(2)}) copy-start(s32[1,1024]{1,0:T(1,128)} %lengths_ref.1) | copy-start | bytes 12292
  8.2 18.8 %collective-permute-start = (f32[256,128]{1,0:T(8,128)S(1)}, f32[256,128]{1,0:T(8,128)S(1)}, u32[]{:S(2)}, u32[]{:S(2)}) collective-permute-start(f32[256,128]{1,0:T(8,128)S(1)} %pool.3.after_ref), channel_id=1, source_target_pairs={{0,8},{4,12},{8,0},{12,4},{1,9},{5,13},{9,1},{13,5},{2,10},{6,14},... | collective-permute-start | bytes 393224 | tf_op jit(solution)/shard_map/ppermute | solution.py:322
  19.2 8.2 %collective-permute-start.1 = (f32[256,128]{1,0:T(8,128)S(1)}, f32[256,128]{1,0:T(8,128)S(1)}, u32[]{:S(2)}, u32[]{:S(2)}) collective-permute-start(f32[256,128]{1,0:T(8,128)S(1)} %get-tuple-element.20), channel_id=1, source_target_pairs={{0,4},{4,8},{8,12},{12,0},{1,5},{5,9},{9,13},{13,1},{2,6},{6,10},{... | collective-permute-start | bytes 393224 | tf_op jit(solution)/shard_map/ppermute | solution.py:322
  20.8 7.6 %copy-start.3 = (bf16[2048,256]{1,0:T(8,128)(2,1)S(1)}, bf16[2048,256]{1,0:T(8,128)(2,1)}, u32[]{:S(2)}) copy-start(bf16[2048,256]{1,0:T(8,128)(2,1)} %refs_4_.1) | copy-start | bytes 3145732
  20.8 13.1 %copy-start = (bf16[2048,512]{1,0:T(8,128)(2,1)S(1)}, bf16[2048,512]{1,0:T(8,128)(2,1)}, u32[]{:S(2)}) copy-start(bf16[2048,512]{1,0:T(8,128)(2,1)} %features_ref.7) | copy-start | bytes 6291460
  20.8 13.1 %copy-start.1 = (bf16[512,1024]{1,0:T(8,128)(2,1)S(1)}, bf16[512,1024]{1,0:T(8,128)(2,1)}, u32[]{:S(2)}) copy-start(bf16[512,1024]{1,0:T(8,128)(2,1)} %w1_ref.7) | copy-start | bytes 3145732
  20.8 13.1 %copy-start.2 = (bf16[1024,256]{1,0:T(8,128)(2,1)S(1)}, bf16[1024,256]{1,0:T(8,128)(2,1)}, u32[]{:S(2)}) copy-start(bf16[1024,256]{1,0:T(8,128)(2,1)} %w2_ref.7) | copy-start | bytes 1572868
  20.9 7.5 %collective-permute-start.2 = (f32[256,128]{1,0:T(8,128)S(1)}, f32[256,128]{1,0:T(8,128)S(1)}, u32[]{:S(2)}, u32[]{:S(2)}) collective-permute-start(f32[256,128]{1,0:T(8,128)S(1)} %get-tuple-element.21.after_ref), channel_id=1, source_target_pairs={{0,12},{4,0},{8,4},{12,8},{1,13},{5,1},{9,5},{13,9},{2,14},{6,2},{... | collective-permute-start | bytes 393224 | tf_op jit(solution)/shard_map/ppermute | solution.py:322
  29.0 13.6 %copy-start.6 = (s32[2048]{0:T(1024)S(1)}, s32[2048]{0:T(1024)}, u32[]{:S(2)}) copy-start(s32[2048]{0:T(1024)} %param.15) | copy-start | bytes 24580
  29.0 1.4 %collective-permute-start.3 = (f32[128,256]{1,0:T(8,128)S(1)}, f32[128,256]{1,0:T(8,128)S(1)}, u32[]{:S(2)}, u32[]{:S(2)}) collective-permute-start(f32[128,256]{1,0:T(8,128)S(1)} %get-tuple-element.23), channel_id=1, source_target_pairs={{0,1},{1,0},{2,3},{3,2},{4,5},{5,4},{6,7},{7,6},{8,9},{9,8},{10,11... | collective-permute-start | bytes 393224 | tf_op jit(solution)/shard_map/ppermute | solution.py:311
  30.4 7.3 %collective-permute-start.6 = (f32[128,256]{1,0:T(8,128)S(1)}, f32[128,256]{1,0:T(8,128)S(1)}, u32[]{:S(2)}, u32[]{:S(2)}) collective-permute-start(f32[128,256]{1,0:T(8,128)S(1)} %add.32), channel_id=1, source_target_pairs={{0,18},{1,19},{2,16},{3,17},{16,2},{17,3},{18,0},{19,1},{4,22},{5,... | collective-permute-start | bytes 393224 | tf_op jit(solution)/shard_map/ppermute | solution.py:317
  32.9 6.9 %collective-permute-start.5 = (f32[128,256]{1,0:T(8,128)S(1)}, f32[128,256]{1,0:T(8,128)S(1)}, u32[]{:S(2)}, u32[]{:S(2)}) collective-permute-start(f32[128,256]{1,0:T(8,128)S(1)} %add.32), channel_id=1, source_target_pairs={{0,16},{1,17},{2,18},{3,19},{16,0},{17,1},{18,2},{19,3},{4,20},{5,... | collective-permute-start | bytes 393224 | tf_op jit(solution)/shard_map/ppermute | solution.py:317
  33.4 6.3 %collective-permute-start.4 = (f32[128,256]{1,0:T(8,128)S(1)}, f32[128,256]{1,0:T(8,128)S(1)}, u32[]{:S(2)}, u32[]{:S(2)}) collective-permute-start(f32[128,256]{1,0:T(8,128)S(1)} %add.32), channel_id=1, source_target_pairs={{0,2},{1,3},{2,0},{3,1},{16,18},{17,19},{18,16},{19,17},{4,6},{5,7... | collective-permute-start | bytes 393224 | tf_op jit(solution)/shard_map/ppermute | solution.py:317
  40.0 2.6 %collective-permute-start.7 = (f32[128,256]{1,0:T(8,128)S(1)}, f32[128,256]{1,0:T(8,128)S(1)}, u32[]{:S(2)}, u32[]{:S(2)}) collective-permute-start(f32[128,256]{1,0:T(8,128)S(1)} %broadcast_multiply_fusion.mine_ref), channel_id=1, source_target_pairs={{0,1},{1,0},{2,3},{3,2},{4,5},{5,4},{6,7},{7,6},{8,9},{9,8},{10,11... | collective-permute-start | bytes 393224 | tf_op jit(solution)/shard_map/ppermute | solution.py:311
  44.4 5.5 %collective-permute-start.10 = (f32[2,2048]{1,0:T(2,128)S(1)}, f32[2,2048]{1,0:T(2,128)S(1)}, u32[]{:S(2)}, u32[]{:S(2)}) collective-permute-start(f32[2,2048]{1,0:T(2,128)S(1)} %get-tuple-element.33), channel_id=1, source_target_pairs={{0,12},{4,8},{8,4},{12,0},{1,13},{5,9},{9,5},{13,1},{2,14},{6,10},... | collective-permute-start | bytes 49160 | tf_op jit(solution)/shard_map/ppermute | solution.py:311
  46.4 4.6 %collective-permute-start.9 = (f32[2,2048]{1,0:T(2,128)S(1)}, f32[2,2048]{1,0:T(2,128)S(1)}, u32[]{:S(2)}, u32[]{:S(2)}) collective-permute-start(f32[2,2048]{1,0:T(2,128)S(1)} %get-tuple-element.33), channel_id=1, source_target_pairs={{0,8},{4,12},{8,0},{12,4},{1,9},{5,13},{9,1},{13,5},{2,10},{6,14},... | collective-permute-start | bytes 49160 | tf_op jit(solution)/shard_map/ppermute | solution.py:311
  46.4 4.6 %collective-permute-start.8 = (f32[2,2048]{1,0:T(2,128)S(1)}, f32[2,2048]{1,0:T(2,128)S(1)}, u32[]{:S(2)}, u32[]{:S(2)}) collective-permute-start(f32[2,2048]{1,0:T(2,128)S(1)} %get-tuple-element.33), channel_id=1, source_target_pairs={{0,4},{4,0},{8,12},{12,8},{1,5},{5,1},{9,13},{13,9},{2,6},{6,2},{1... | collective-permute-start | bytes 49160 | tf_op jit(solution)/shard_map/ppermute | solution.py:311
where the time goes:
time: 51.9 us; the launch traced here: 51.7 us
  Pallas kernels  25.6 us (49%)
  starting transfers between devices  16.1 us (31%)
  waiting for transfers between devices  8.3 us (16%)
  other arithmetic  0.86 us (2%)
  between operations  0.82 us (2%)
    pallas_call x3, Pallas kernels, pool(): pl.pallas_call(functools.partial(pool_kernel, positions, aheads), out_sha...  14.6 us
    ppermute x3, starting transfers between devices, shift(): return lax.ppermute(x, axis, [(i, (i + by) % size) for i in range(size)])  8.06 us
    pallas_call x4, Pallas kernels, tower(): pl.pallas_call(functools.partial(tower_kernel, min(256, users)), grid=(1,...  4.96 us
    ppermute x5, starting transfers between devices, swap(): lax.ppermute(x, axis, [(i, i ^ bit) for i in range(lax.axis_size(axis))])  4.53 us
    pallas_call x1, Pallas kernels, widen(): pl.pallas_call(functools.partial(widen_kernel, pieces), out_shape=pltpu.V...  3.63 us
    ppermute x5, waiting for transfers between devices, swap(): lax.ppermute(x, axis, [(i, i ^ bit) for i in range(lax.axis_size(axis))])  3.61 us
    ppermute x3, starting transfers between devices, swap_both(): return lax.ppermute(x, ('tab', 'dp'), pairs)  3.55 us
    ppermute x3, waiting for transfers between devices, swap_both(): return lax.ppermute(x, ('tab', 'dp'), pairs)  3.33 us
  transfers between devices with their start and end apart: 11, of which 7 were waited for; matrix products, arithmetic and copies ran while one was open for 0% of the time, Pallas kernels for 30%

commit v1 on v0

v1 whole, which is shorter than its diff:
```python
import functools

import jax
import jax.numpy as jnp
from jax import lax
from jax.experimental import pallas as pl
from jax.experimental.pallas import tpu as pltpu
from jax.sharding import PartitionSpec as P


epsilon = 1e-06
logit_scale = 20.0
log2_e = 1.4426950408889634
ln_2 = 0.6931471805599453


f32 = jnp.float32
bf16 = jnp.bfloat16
VMEM = pl.BlockSpec(memory_space=pltpu.VMEM)
SMEM = pl.BlockSpec(memory_space=pltpu.SMEM)
ANY = pl.BlockSpec(memory_space=pl.ANY)
MIB = 1 << 20
zero_rows = 8
bags_at_once = 16
tower_parts = 4


def widen_kernel(pieces, table_ref, wide_ref, raw, sems):
    rows = table_ref.shape[0]
    piece = rows // pieces
    block = min(1024, piece)
    copies = [
        pltpu.make_async_copy(
            table_ref.at[pl.ds(k * piece, piece)], raw.at[pl.ds(k * piece, piece)], sems.at[k]
        )
        for k in range(pieces)
    ]
    for copy in copies:
        copy.start()
    wide_ref[pl.ds(rows, zero_rows), :] = jnp.zeros((zero_rows, wide_ref.shape[1]), f32)
    for k in range(pieces):
        copies[k].wait()

        @pl.loop(0, piece // block)
        def _(i):
            at = pl.ds(pl.multiple_of(k * piece + i * block, block), block)
            wide_ref[at, :] = raw[at, :].astype(f32)


def widen(table):
    rows, width = table.shape
    pieces = 16
    return pl.pallas_call(
        functools.partial(widen_kernel, pieces),
        out_shape=pltpu.VMEM((rows + zero_rows, width), f32),
        in_specs=[pl.BlockSpec(memory_space=pltpu.HBM)],
        out_specs=VMEM,
        scratch_shapes=[pltpu.VMEM((rows, width), bf16), pltpu.SemaphoreType.DMA((pieces,))],
        compiler_params=pltpu.CompilerParams(vmem_limit_bytes=30 * MIB),
        cost_estimate=pl.CostEstimate(flops=10**6, bytes_accessed=rows * width * 2, transcendentals=0),
        name="widen",
    )(table)


def place_kernel(T, C, rows, ids_ref, lengths_ref, after_ref, places_ref, inverse_ref):
    positions, items = ids_ref.shape
    run = items // (T * C)
    local = ids_ref[...] - lax.axis_index("tab") * rows
    valid = lax.broadcasted_iota(jnp.int32, local.shape, 0) < lengths_ref[...]
    places = jnp.where((local >= 0) & (local < rows) & valid, local, rows)
    inverse = 1.0 / lengths_ref[...].astype(f32)
    for t in range(T):
        for c in range(C):
            at = (t * C + c) * run
            to = pl.ds((c * T + t) * positions, positions)
            places_ref[to, :] = places[:, at : at + run]
            inverse_ref[pl.ds(c * T + t, 1), :] = inverse[:, at : at + run]


def place(ids, lengths, wide, T, C):
    positions, items = ids.shape
    rows = wide.shape[0] - zero_rows
    run = items // (T * C)
    if run % 128 == 0:
        places, inverse = pl.pallas_call(
            functools.partial(place_kernel, T, C, rows),
            out_shape=(
                jax.ShapeDtypeStruct((C * positions * T, run), jnp.int32),
                jax.ShapeDtypeStruct((C * T, run), f32),
            ),
            in_specs=[VMEM, VMEM, ANY],
            out_specs=(VMEM, VMEM),
            compiler_params=pltpu.CompilerParams(vmem_limit_bytes=4 * MIB),
            name="place",
        )(ids, lengths, wide)
        return places.reshape(-1), inverse.reshape(-1)
    local = ids - lax.axis_index("tab") * rows
    valid = lax.broadcasted_iota(jnp.int32, ids.shape, 0) < lengths
    places = jnp.where((local >= 0) & (local < rows) & valid, local, rows)
    places = places.reshape(positions, T, C, run).transpose(2, 1, 0, 3).reshape(-1)
    inverse = (1.0 / lengths.astype(f32)).reshape(T, C, run).transpose(1, 0, 2).reshape(-1)
    return places, inverse


def pool_kernel(positions, run, ahead, inverse_ref, wide_ref, places_ref, after_ref, out_ref, *refs):
    places, inverse, sems = refs
    count = out_ref.shape[0]
    size = count * positions
    pieces = sems.shape[0] - 1
    chunk = lax.rem(lax.axis_index("cand") + ahead, lax.axis_size("cand"))
    copies = [pltpu.make_async_copy(inverse_ref, inverse, sems.at[pieces])]
    for k in range(pieces):
        piece = size // pieces
        start = pl.multiple_of(chunk * size + k * piece, piece)
        copies.append(
            pltpu.make_async_copy(
                places_ref.at[pl.ds(start, piece)], places.at[pl.ds(k * piece, piece)], sems.at[k]
            )
        )
    for copy in copies:
        copy.start()
    copies[0].wait()
    at_once = min(bags_at_once, run)
    for t in range(count // run):
        if t < pieces:
            copies[t + 1].wait()
        index_refs = [places.at[pl.ds((t * positions + p) * run, run)] for p in range(positions)]

        @pl.loop(0, run // at_once)
        def _(b):
            for u in range(at_once):
                i = b * at_once + u
                rows = [wide_ref[pl.ds(ref[i], 1), :] for ref in index_refs]
                while len(rows) > 1:
                    rows = [sum(rows[n : n + 2][1:], rows[n]) for n in range(0, len(rows), 2)]
                scale = inverse[chunk * count + t * run + i]
                out_ref[pl.ds(t * run + i, 1), :] = rows[0] * scale


def pool(ahead, inverse, wide, places, after, count, positions, run):
    width = wide.shape[1]
    pieces = count // run if positions * run % 1024 == 0 else 1
    return pl.pallas_call(
        functools.partial(pool_kernel, positions, run, ahead),
        out_shape=jax.ShapeDtypeStruct((count, width), f32),
        in_specs=[ANY, VMEM, ANY, ANY],
        out_specs=VMEM,
        scratch_shapes=[
            pltpu.SMEM((count * positions,), jnp.int32),
            pltpu.SMEM(inverse.shape, f32),
            pltpu.SemaphoreType.DMA((pieces + 1,)),
        ],
        compiler_params=pltpu.CompilerParams(vmem_limit_bytes=20 * MIB),
        cost_estimate=pl.CostEstimate(
            flops=10**7, bytes_accessed=count * width * 4, transcendentals=0
        ),
        name="pool",
    )(inverse, wide, places, after)


def project_kernel(order, other, *refs):
    count = len(order)
    parts, weight_ref, out_ref = refs[:count], refs[count], refs[-1]
    half = out_ref.shape[0]
    width = parts[0].shape[1]
    c, d = lax.axis_index("cand"), lax.axis_index("dp")
    C, D = lax.axis_size("cand"), lax.axis_size("dp")
    which = lax.rem(d + other, 2)
    at = pl.ds(pl.multiple_of(which * half, half), half)
    total = None
    for k in range(count):
        value = parts[k][at, :]
        source = lax.rem(c + C - order[k], C) * D + d
        weight = weight_ref[pl.ds(pl.multiple_of(source * width, width), width), :]
        for _ in range(3):
            short = value.astype(bf16)
            term = jnp.dot(short, weight, preferred_element_type=f32)
            total = term if total is None else total + term
            value = value - short.astype(f32)
    out_ref[...] = total


def project(order, other, parts, weight, after):
    rows = parts[0].shape[0]
    return pl.pallas_call(
        functools.partial(project_kernel, order, other),
        out_shape=jax.ShapeDtypeStruct((rows // 2, weight.shape[1]), f32),
        in_specs=[VMEM] * (len(parts) + 1) + [ANY] * len(after),
        out_specs=VMEM,
        compiler_params=pltpu.CompilerParams(vmem_limit_bytes=8 * MIB),
        cost_estimate=pl.CostEstimate(flops=10**8, bytes_accessed=2 * MIB, transcendentals=0),
        name="project",
    )(*parts, weight, *after)


def tower_kernel(block, features_ref, w1_ref, w2_ref, after_ref, high_ref, low_ref):
    for start in range(0, features_ref.shape[0], block):
        at = pl.ds(start, block)
        hidden = jnp.dot(features_ref[at, :], w1_ref[...], preferred_element_type=f32)
        hidden = 0.5 * hidden * (1.0 + lax.erf(hidden * (0.5**0.5)))
        emb = jnp.dot(hidden.astype(bf16), w2_ref[...], preferred_element_type=f32)
        emb = emb * lax.rsqrt(jnp.mean(emb * emb, axis=1, keepdims=True) + epsilon)
        high = emb.astype(bf16)
        high_ref[at, :] = high
        low_ref[at, :] = (emb - high.astype(f32)).astype(bf16)


def tower(part, parts, features, w1, w2, after):
    users = features.shape[0] // parts
    embed = w2.shape[1]
    whole = lambda i: (0, 0)
    shape = jax.ShapeDtypeStruct((users, embed), bf16)
    return pl.pallas_call(
        functools.partial(tower_kernel, min(256, users)),
        grid=(1,),
        out_shape=(shape, shape),
        in_specs=[
            pl.BlockSpec((users, features.shape[1]), lambda i: (part, 0)),
            VMEM,
            VMEM,
            ANY,
        ],
        out_specs=(pl.BlockSpec((users, embed), whole), pl.BlockSpec((users, embed), whole)),
        compiler_params=pltpu.CompilerParams(vmem_limit_bytes=16 * MIB),
        cost_estimate=pl.CostEstimate(
            flops=2 * users * (w1.size + w2.size), bytes_accessed=2 * MIB, transcendentals=users * w1.shape[1]
        ),
    )(features, w1, w2, after)


def split(x, size):
    if size & (size - 1) == 0:
        return x >> (size.bit_length() - 1), x & (size - 1)
    return lax.div(x, jnp.full_like(x, size)), lax.rem(x, jnp.full_like(x, size))


def unit_rows(rows):
    return rows * lax.rsqrt(jnp.mean(rows * rows, axis=1, keepdims=True) + epsilon)


def scores_kernel(count, block, own, other, positive_ref, mine_ref, *refs):
    t, c, d = (lax.axis_index(axis) for axis in ("tab", "cand", "dp"))
    C, D = lax.axis_size("cand"), lax.axis_size("dp")
    half = mine_ref.shape[0]
    first = lax.rem(d + other, 2) * half
    emb = unit_rows(mine_ref[...])
    items = emb * (logit_scale / emb.shape[1] * log2_e)
    item_high = items.astype(bf16)
    item_low = (items - item_high.astype(f32)).astype(bf16)
    users = refs[0].shape[0]
    out_ref = refs[-1]
    if other:
        before_ref, earlier_ref, item_ref, out_ref, emb_ref = refs[-5:]
        emb_ref[pl.ds(0, half), :] = emb
        emb_ref[pl.ds(half, half), :] = unit_rows(earlier_ref[...])

    def dot(a, b):
        return lax.dot_general(a, b, (((1,), (1,)), ((), ())), preferred_element_type=f32)

    for k in range(count):
        high_ref, low_ref = refs[2 * k], refs[2 * k + 1]
        for start in range(0, users, block):
            at = pl.ds(start, block)
            high = high_ref[at, :]
            scores = dot(item_high, high) + (dot(item_low, high) + dot(item_high, low_ref[at, :]))
            to = pl.ds(k * users + start, block)
            rest, within = split(positive_ref[:, to], own)
            rest, owner_d = split(rest, D)
            owner_t, owner_c = split(rest, C)
            place = (owner_t * D + owner_d) * own + within - first
            place = jnp.where(owner_c == c, place, -1)
            here = lax.broadcasted_iota(jnp.int32, scores.shape, 0) == place
            total = jnp.sum(jnp.exp2(scores), axis=0, keepdims=True)
            positive = jnp.sum(jnp.where(here, scores, 0.0), axis=0, keepdims=True)
            if other:
                total = total + before_ref[pl.ds(0, 1), to]
                positive = positive + before_ref[pl.ds(1, 1), to]
            out_ref[pl.ds(0, 1), to] = total
            out_ref[pl.ds(1, 1), to] = positive
    if other:
        row = (t * D + d) * own - first
        row = jnp.where(row < 0, row + 2 * half, row)
        step = 8 if own % 8 == 0 else 1
        for k in range(0, own, step):
            item_ref[pl.ds(k, step), :] = emb_ref[pl.ds(pl.multiple_of(row + k, step), step), :]


def score(positives, rows, embs, own, earlier=()):
    count = len(embs)
    users = embs[0][0].shape[0]
    flat = [x for pair in embs for x in pair] + list(earlier)
    total = users * count
    other = len(earlier) // 2
    item = (jax.ShapeDtypeStruct((own, rows.shape[1]), f32),) * other
    return pl.pallas_call(
        functools.partial(scores_kernel, count, min(512, users), own, other),
        out_shape=item + (jax.ShapeDtypeStruct((2, total), f32),),
        in_specs=[VMEM] * (2 + len(flat)),
        out_specs=(VMEM,) * (1 + other),
        scratch_shapes=[pltpu.VMEM((2 * rows.shape[0], rows.shape[1]), f32)] * other,
        compiler_params=pltpu.CompilerParams(vmem_limit_bytes=16 * MIB),
        cost_estimate=pl.CostEstimate(
            flops=6 * total * rows.shape[1] * rows.shape[0], bytes_accessed=2 * MIB, transcendentals=0
        ),
    )(positives, rows, *flat)


def finish_kernel(*refs):
    total = refs[0][...]
    for ref in refs[1:-1]:
        total = total + ref[...]
    refs[-1][...] = (jnp.log2(total[:1]) - total[1:]) * ln_2


def finish(partials):
    return pl.pallas_call(
        finish_kernel,
        out_shape=jax.ShapeDtypeStruct((1, partials[0].shape[1]), f32),
        in_specs=[VMEM] * len(partials),
        out_specs=VMEM,
        compiler_params=pltpu.CompilerParams(vmem_limit_bytes=4 * MIB),
        name="finish",
    )(*partials).reshape(-1)


def swap(x, axis, bit):
    return lax.ppermute(x, axis, [(i, i ^ bit) for i in range(lax.axis_size(axis))])


def swap_both(x, bit_dp, bit_tab):
    T, D = lax.axis_size("tab"), lax.axis_size("dp")
    pairs = [(t * D + d, (t ^ bit_tab) * D + (d ^ bit_dp)) for t in range(T) for d in range(D)]
    return lax.ppermute(x, ("tab", "dp"), pairs)


def shift(x, axis, by):
    size = lax.axis_size(axis)
    return lax.ppermute(x, axis, [(i, (i + by) % size) for i in range(size)])


def bits_of(axis):
    return [(axis, 1 << k) for k in range(lax.axis_size(axis).bit_length() - 1)]


def body(
    tables, bag_ids, bag_lengths, item_weight, user_features, user_w1, user_w2, positive_items
):
    table = tables[0]
    ids = bag_ids[0].T
    T, C, D = lax.axis_size("tab"), lax.axis_size("cand"), lax.axis_size("dp")
    positions, items = ids.shape
    own = items // (T * C * D)
    count = items // C

    wide = widen(table)
    places, inverse = place(ids, bag_lengths, wide, T, C)
    order = pool_order(C)
    after = places
    received = []
    for j in order:
        part = pool(j, inverse, wide, places, after, count, positions, items // (T * C))
        after = part
        if j:
            part = shift(part, "cand", j)
        received.append(part)

    send = project(order, 1, received, item_weight, ())
    came = swap(send, "dp", 1)
    keep = project(order, 0, received, item_weight, (send,))
    total = keep + came
    embs = []
    for k in range(tower_parts):
        embs.append(tower(k, tower_parts, user_features, user_w1, user_w2, send))
    steps = [step for step in bits_of("dp") if step[1] > 1] + bits_of("tab")
    if len(steps) == 2:
        moved = []
        for picked in ((1, 1), (1, 0), (0, 1)):
            moved.append(swap_both(total, picked[0] * steps[0][1], picked[1] * steps[1][1]))
        total = (total + moved[1]) + (moved[2] + moved[0])
    else:
        for step in steps:
            total = total + swap(total, *step)
    positives = positive_items[None]
    other = swap(total, "dp", 1)
    (partial,) = score(positives, total, embs, own)
    item_emb, partial = score(positives, other, embs, own, (partial, total))
    partials = [partial]
    for j in range(1, C):
        partials.append(swap(partial, "cand", j))
    return (item_emb, finish(partials))


def pool_order(C):
    return tuple(range(C - 1, -1, -1))


def solution(mesh):
    placed = (
        P(("cand", "dp"), "tab", None),
        P(("cand", "dp"), None, None),
        P(("cand", "dp"), None),
        P(),
        P(("tab", "dp"), None),
        P(),
        P(),
        P(("tab", "dp")),
    )
    return jax.shard_map(
        body,
        mesh=mesh,
        in_specs=placed,
        out_specs=(P(("tab", "cand", "dp"), None), P(("tab", "dp"))),
        check_vma=False,
    )
```

time: 51.9 us -> 55.6 us (1.071)
  waiting for transfers between devices: 8.3 us -> 12 us
  Pallas kernels: 25.6 us -> 26.8 us
  other arithmetic: 0.86 us -> 0.05 us
    ppermute x3, waiting for transfers between devices: 1.36 us -> 3.7 us  [shift(): return lax.ppermute(x, axis, [(i, (i + by) % size) for i in range(size)])]
    ppermute x5, waiting for transfers between devices: 3.61 us -> 4.95 us  [swap(): lax.ppermute(x, axis, [(i, i ^ bit) for i in range(lax.axis_size(axis))])]
    ppermute x3, starting transfers between devices: 8.06 us -> 7.04 us  [shift(): return lax.ppermute(x, axis, [(i, (i + by) % size) for i in range(size)])]
    mul x2 -> x0, other arithmetic: 0.71 us -> none  [the longest x1 0.62 us: body(): user_loss = (jnp.log2(summed[0]) - summed[1]) * ln_2]
    pallas_call x1 -> x2, Pallas kernels: 1.81 us -> 2.49 us  [score(): pl.pallas_call(functools.partial(scores_kernel, count, min(512, users), o...]
    ppermute x5, starting transfers between devices: 4.53 us -> 5.19 us  [swap(): lax.ppermute(x, axis, [(i, i ^ bit) for i in range(lax.axis_size(axis))])]
    pallas_call x4 -> x7, Pallas kernels: 15.1 us -> 15.7 us  [the longest x4 14.3 us: pool(): pl.pallas_call(functools.partial(pool_kernel, positions, run, ahead), out...]
  transfers between devices with their start and end apart: 11 -> 11, of which waited for: 7 -> 6; matrix products, arithmetic and copies ran while one was open for 0% -> 0% of each run, Pallas kernels for 30% -> 18%
where the time goes in v1:
time: 55.6 us; the launch traced here: 55.5 us
  Pallas kernels  26.8 us (48%)
  starting transfers between devices  15.8 us (28%)
  waiting for transfers between devices  12 us (22%)
  between operations  0.86 us (2%)
    pallas_call x4, Pallas kernels, pool(): pl.pallas_call(functools.partial(pool_kernel, positions, run, ahead), out...  14.3 us
    ppermute x3, starting transfers between devices, shift(): return lax.ppermute(x, axis, [(i, (i + by) % size) for i in range(size)])  7.04 us
    ppermute x5, starting transfers between devices, swap(): lax.ppermute(x, axis, [(i, i ^ bit) for i in range(lax.axis_size(axis))])  5.19 us
    pallas_call x4, Pallas kernels, tower(): pl.pallas_call(functools.partial(tower_kernel, min(256, users)), grid=(1,...  4.96 us
    ppermute x5, waiting for transfers between devices, swap(): lax.ppermute(x, axis, [(i, i ^ bit) for i in range(lax.axis_size(axis))])  4.95 us
    ppermute x3, waiting for transfers between devices, shift(): return lax.ppermute(x, axis, [(i, (i + by) % size) for i in range(size)])  3.7 us
    pallas_call x1, Pallas kernels, widen(): pl.pallas_call(functools.partial(widen_kernel, pieces), out_shape=pltpu.V...  3.61 us
    ppermute x3, starting transfers between devices, swap_both(): return lax.ppermute(x, ('tab', 'dp'), pairs)  3.55 us
  transfers between devices with their start and end apart: 11, of which 6 were waited for; matrix products, arithmetic and copies ran while one was open for 0% of the time, Pallas kernels for 18%

profile of v1, /device:TPU:0, one launch (start us, length us, event | category | flops | bytes accessed | tf_op | source)
XLA Modules:
  0.0 55.5 jit_solution(5684166149703714521)
XLA Ops:
  0.6 0.0 copy-start.4
  0.6 0.0 copy-start.6
  0.6 3.6 %widen.1.after_ref.wide_ref = f32[32776,128]{1,0:T(8,128)S(1)} custom-call(bf16[32768,128]{1,0:T(8,128)(2,1)} %bitcast.20), custom_call_target="tpu_custom_call" | custom-call | flops 1000000 | bytes 8388608 | tf_op jit(solution)/shard_map/widen/pallas_call | solution.py:53
  4.3 0.0 copy-done.4
  4.3 0.0 copy-done.6
  4.3 3.6 %pool.4.after_ref = f32[256,128]{1,0:T(8,128)S(1)} custom-call(f32[1024]{0:T(1024)S(1)} %bitcast.14, f32[32776,128]{1,0:T(8,128)S(1)} %widen.1.after_ref.wide_ref, s32[16384]{0:T(1024)S(1)} %bitcast.8, s32[16384]{0:T(1024)S(1)} %bitcast.9), custom_call_target="tpu_custom_call" | custom-call | flops 10000000 | bytes 131072 | tf_op jit(solution)/shard_map/pool/pallas_call | solution.py:143
  7.9 3.6 %pool.5.after_ref = f32[256,128]{1,0:T(8,128)S(1)} custom-call(f32[1024]{0:T(1024)S(1)} %bitcast.15, f32[32776,128]{1,0:T(8,128)S(1)} %widen.1.after_ref.wide_ref, s32[16384]{0:T(1024)S(1)} %bitcast.10, f32[256,128]{1,0:T(8,128)S(1)} %pool.4.after_ref), custom_call_target="tpu_custom_call" | custom-call | flops 10000000 | bytes 131072 | tf_op jit(solution)/shard_map/pool/pallas_call | solution.py:143
  11.5 3.6 %pool.6.after_ref = f32[256,128]{1,0:T(8,128)S(1)} custom-call(f32[1024]{0:T(1024)S(1)} %bitcast.16, f32[32776,128]{1,0:T(8,128)S(1)} %widen.1.after_ref.wide_ref, s32[16384]{0:T(1024)S(1)} %bitcast.11, f32[256,128]{1,0:T(8,128)S(1)} %pool.5.after_ref), custom_call_target="tpu_custom_call" | custom-call | flops 10000000 | bytes 131072 | tf_op jit(solution)/shard_map/pool/pallas_call | solution.py:143
  15.1 0.0 copy-start.3
  15.1 0.0 copy-start
  15.1 0.0 copy-start.1
  15.1 0.0 copy-start.2
  15.2 3.1 %collective-permute-start.2 = (f32[256,128]{1,0:T(8,128)S(1)}, f32[256,128]{1,0:T(8,128)S(1)}, u32[]{:S(2)}, u32[]{:S(2)}) collective-permute-start(f32[256,128]{1,0:T(8,128)S(1)} %pool.6.after_ref), channel_id=1, source_target_pairs={{0,4},{4,8},{8,12},{12,0},{1,5},{5,9},{9,13},{13,1},{2,6},{6,10},{... | collective-permute-start | bytes 393224 | tf_op jit(solution)/shard_map/ppermute | solution.py:338
  18.3 2.6 %collective-permute-start.1 = (f32[256,128]{1,0:T(8,128)S(1)}, f32[256,128]{1,0:T(8,128)S(1)}, u32[]{:S(2)}, u32[]{:S(2)}) collective-permute-start(f32[256,128]{1,0:T(8,128)S(1)} %pool.5.after_ref), channel_id=1, source_target_pairs={{0,8},{4,12},{8,0},{12,4},{1,9},{5,13},{9,1},{13,5},{2,10},{6,14},... | collective-permute-start | bytes 393224 | tf_op jit(solution)/shard_map/ppermute | solution.py:338
  20.8 1.3 %collective-permute-start = (f32[256,128]{1,0:T(8,128)S(1)}, f32[256,128]{1,0:T(8,128)S(1)}, u32[]{:S(2)}, u32[]{:S(2)}) collective-permute-start(f32[256,128]{1,0:T(8,128)S(1)} %pool.4.after_ref), channel_id=1, source_target_pairs={{0,12},{4,0},{8,4},{12,8},{1,13},{5,1},{9,5},{13,9},{2,14},{6,2},{... | collective-permute-start | bytes 393224 | tf_op jit(solution)/shard_map/ppermute | solution.py:338
  22.2 3.6 %pool.7.refs_3_ = f32[256,128]{1,0:T(8,128)S(1)} custom-call(f32[1024]{0:T(1024)S(1)} %bitcast.17, f32[32776,128]{1,0:T(8,128)S(1)} %widen.1.after_ref.wide_ref, s32[16384]{0:T(1024)S(1)} %bitcast.12, f32[256,128]{1,0:T(8,128)S(1)} %pool.6.after_ref), custom_call_target="tpu_custom_call" | custom-call | flops 10000000 | bytes 131072 | tf_op jit(solution)/shard_map/pool/pallas_call | solution.py:143
  25.8 0.0 collective-permute-done.2.refs_2_
  25.8 3.7 %collective-permute-done.1.refs_1_ = f32[256,128]{1,0:T(8,128)S(1)} collective-permute-done((f32[256,128]{1,0:T(8,128)S(1)}, f32[256,128]{1,0:T(8,128)S(1)}, u32[]{:S(2)}, u32[]{:S(2)}) %collective-permute-start.1) | collective-permute-done | bytes 131104 | tf_op jit(solution)/shard_map/ppermute | solution.py:338
  29.5 0.0 collective-permute-done.refs_0_
  29.5 0.0 copy-done.3
  29.5 0.4 project.2.refs_5_.after_ref
  29.9 0.1 collective-permute-start.3
  29.9 0.4 project.3
  30.3 0.0 copy-start.5
  30.3 0.9 %collective-permute-done.3 = f32[128,256]{1,0:T(8,128)S(1)} collective-permute-done((f32[128,256]{1,0:T(8,128)S(1)}, f32[128,256]{1,0:T(8,128)S(1)}, u32[]{:S(2)}, u32[]{:S(2)}) %collective-permute-start.3) | collective-permute-done | bytes 131104 | tf_op jit(solution)/shard_map/ppermute | solution.py:327
  31.3 2.5 %collective-permute-start.6 = (f32[128,256]{1,0:T(8,128)S(1)}, f32[128,256]{1,0:T(8,128)S(1)}, u32[]{:S(2)}, u32[]{:S(2)}) collective-permute-start(f32[128,256]{1,0:T(8,128)S(1)} %add.12), channel_id=1, source_target_pairs={{0,18},{1,19},{2,16},{3,17},{16,2},{17,3},{18,0},{19,1},{4,22},{5,... | collective-permute-start | bytes 393224 | tf_op jit(solution)/shard_map/ppermute | solution.py:333
  33.8 0.5 collective-permute-start.5
  34.3 0.5 collective-permute-start.4
  34.8 0.0 copy-done
  34.9 0.0 copy-done.1
  34.9 0.0 copy-done.2
  34.9 1.2 %shard_map.98 = (bf16[512,256]{1,0:T(8,128)(2,1)S(1)}, bf16[512,256]{1,0:T(8,128)(2,1)S(1)}) custom-call(bf16[2048,512]{1,0:T(8,128)(2,1)S(1)} %copy-done, bf16[512,1024]{1,0:T(8,128)(2,1)S(1)} %copy-done.1, bf16[1024,256]{1,0:T(8,128)(2,1)S(1)} %copy-done.2, f32[128,256]{1,0:T(8,128)S(1)} %project.2.refs_5_.after_ref), custom_call_target="tpu_custom_call" | custom-call | flops 805306368 | bytes 2097152 | tf_op jit(solution)/shard_map/pallas_call | solution.py:213
  36.1 1.2 %shard_map.97 = (bf16[512,256]{1,0:T(8,128)(2,1)S(1)}, bf16[512,256]{1,0:T(8,128)(2,1)S(1)}) custom-call(bf16[2048,512]{1,0:T(8,128)(2,1)S(1)} %copy-done, bf16[512,1024]{1,0:T(8,128)(2,1)S(1)} %copy-done.1, bf16[1024,256]{1,0:T(8,128)(2,1)S(1)} %copy-done.2, f32[128,256]{1,0:T(8,128)S(1)} %project.2.refs_5_.after_ref), custom_call_target="tpu_custom_call" | custom-call | flops 805306368 | bytes 2097152 | tf_op jit(solution)/shard_map/pallas_call | solution.py:213
  37.3 1.3 %collective-permute-done.6 = f32[128,256]{1,0:T(8,128)S(1)} collective-permute-done((f32[128,256]{1,0:T(8,128)S(1)}, f32[128,256]{1,0:T(8,128)S(1)}, u32[]{:S(2)}, u32[]{:S(2)}) %collective-permute-start.6) | collective-permute-done | bytes 131104 | tf_op jit(solution)/shard_map/ppermute | solution.py:333
  38.6 2.0 %collective-permute-done.5 = f32[128,256]{1,0:T(8,128)S(1)} collective-permute-done((f32[128,256]{1,0:T(8,128)S(1)}, f32[128,256]{1,0:T(8,128)S(1)}, u32[]{:S(2)}, u32[]{:S(2)}) %collective-permute-start.5) | collective-permute-done | bytes 131104 | tf_op jit(solution)/shard_map/ppermute | solution.py:333
  40.7 0.0 collective-permute-done.4
  40.7 0.1 collective-permute-start.7
  40.8 1.2 %shard_map.96 = (bf16[512,256]{1,0:T(8,128)(2,1)S(1)}, bf16[512,256]{1,0:T(8,128)(2,1)S(1)}) custom-call(bf16[2048,512]{1,0:T(8,128)(2,1)S(1)} %copy-done, bf16[512,1024]{1,0:T(8,128)(2,1)S(1)} %copy-done.1, bf16[1024,256]{1,0:T(8,128)(2,1)S(1)} %copy-done.2, f32[128,256]{1,0:T(8,128)S(1)} %project.2.refs_5_.after_ref), custom_call_target="tpu_custom_call" | custom-call | flops 805306368 | bytes 2097152 | tf_op jit(solution)/shard_map/pallas_call | solution.py:213
  42.0 1.2 %shard_map.95 = (bf16[512,256]{1,0:T(8,128)(2,1)S(1)}, bf16[512,256]{1,0:T(8,128)(2,1)S(1)}) custom-call(bf16[2048,512]{1,0:T(8,128)(2,1)S(1)} %copy-done, bf16[512,1024]{1,0:T(8,128)(2,1)S(1)} %copy-done.1, bf16[1024,256]{1,0:T(8,128)(2,1)S(1)} %copy-done.2, f32[128,256]{1,0:T(8,128)S(1)} %project.2.refs_5_.after_ref), custom_call_target="tpu_custom_call" | custom-call | flops 805306368 | bytes 2097152 | tf_op jit(solution)/shard_map/pallas_call | solution.py:213
  43.3 0.0 copy-done.5
  43.3 1.2 %shard_map.99.refs_8_ = f32[2,2048]{1,0:T(2,128)S(1)} custom-call(s32[1,2048]{1,0:T(1,128)S(1)} %bitcast.18, f32[128,256]{1,0:T(8,128)S(1)} %add_add_fusion.mine_ref.refs_9_, bf16[512,256]{1,0:T(8,128)(2,1)S(1)} %get-tuple-element.16.refs_0_, bf16[512,256]{1,0:T(8,128)(2,1)S(1)} %get-tuple-element.17.refs_1_, ...), custom_call_target="tpu_custom_call" | custom-call | flops 402653184 | bytes 2097152 | tf_op jit(solution)/shard_map/pallas_call | solution.py:295
  44.5 0.0 collective-permute-done.7.mine_ref
  44.6 1.2 %shard_map.100 = (f32[32,256]{1,0:T(8,128)}, f32[2,2048]{1,0:T(2,128)S(1)}) custom-call(s32[1,2048]{1,0:T(1,128)S(1)} %bitcast.19, f32[128,256]{1,0:T(8,128)S(1)} %collective-permute-done.7.mine_ref, bf16[512,256]{1,0:T(8,128)(2,1)S(1)} %get-tuple-element.16.refs_0_, bf16[512,256]{1,0:T(8,128)(2,1)S(1)} %get-tuple-element.17.refs_1_, ...), custom_call_target="tpu_custom_call" | custom-call | flops 402653184 | bytes 2097152 | tf_op jit(solution)/shard_map/pallas_call | solution.py:295
  45.8 4.4 %collective-permute-start.10 = (f32[2,2048]{1,0:T(2,128)S(1)}, f32[2,2048]{1,0:T(2,128)S(1)}, u32[]{:S(2)}, u32[]{:S(2)}) collective-permute-start(f32[2,2048]{1,0:T(2,128)S(1)} %get-tuple-element.25.refs_0_), channel_id=1, source_target_pairs={{0,12},{4,8},{8,4},{12,0},{1,13},{5,9},{9,5},{13,1},{2,14},{6,10},... | collective-permute-start | bytes 49160 | tf_op jit(solution)/shard_map/ppermute | solution.py:327
  50.2 0.4 collective-permute-start.9
  50.6 0.2 collective-permute-start.8
  50.9 1.1 %collective-permute-done.10.refs_3_ = f32[2,2048]{1,0:T(2,128)S(1)} collective-permute-done((f32[2,2048]{1,0:T(2,128)S(1)}, f32[2,2048]{1,0:T(2,128)S(1)}, u32[]{:S(2)}, u32[]{:S(2)}) %collective-permute-start.10) | collective-permute-done | bytes 16416 | tf_op jit(solution)/shard_map/ppermute | solution.py:327
  52.0 2.9 %collective-permute-done.9.refs_2_ = f32[2,2048]{1,0:T(2,128)S(1)} collective-permute-done((f32[2,2048]{1,0:T(2,128)S(1)}, f32[2,2048]{1,0:T(2,128)S(1)}, u32[]{:S(2)}, u32[]{:S(2)}) %collective-permute-start.9) | collective-permute-done | bytes 16416 | tf_op jit(solution)/shard_map/ppermute | solution.py:327
  54.9 0.0 collective-permute-done.8.refs_1_
  54.9 0.6 %finish.1 = f32[1,2048]{1,0:T(1,128)} custom-call(f32[2,2048]{1,0:T(2,128)S(1)} %get-tuple-element.25.refs_0_, f32[2,2048]{1,0:T(2,128)S(1)} %collective-permute-done.8.refs_1_, f32[2,2048]{1,0:T(2,128)S(1)} %collective-permute-done.9.refs_2_, f32[2,2048]{1,0:T(2,128)S(1)} %collective-permute-done.10.refs_3_), custom_call_target="tpu_custom_call" | custom-call | tf_op jit(solution)/shard_map/finish/pallas_call | solution.py:316
  (3 shorter events, 0.1 us)
Async XLA Ops:
  0.6 3.6 %copy-start.4 = (s32[1,1024,16]{1,2,0:T(8,128)S(1)}, s32[1,1024,16]{1,2,0:T(8,128)}, u32[]{:S(2)}) copy-start(s32[1,1024,16]{1,2,0:T(8,128)} %param.9) | copy-start | bytes 196612
  0.6 3.6 %copy-start.6 = (s32[1,1024]{1,0:T(1,128)S(1)}, s32[1,1024]{1,0:T(1,128)}, u32[]{:S(2)}) copy-start(s32[1,1024]{1,0:T(1,128)} %lengths_ref.1) | copy-start | bytes 12292
  15.1 14.4 %copy-start.3 = (bf16[2048,256]{1,0:T(8,128)(2,1)S(1)}, bf16[2048,256]{1,0:T(8,128)(2,1)}, u32[]{:S(2)}) copy-start(bf16[2048,256]{1,0:T(8,128)(2,1)} %refs_4_.3) | copy-start | bytes 3145732
  15.1 19.7 %copy-start = (bf16[2048,512]{1,0:T(8,128)(2,1)S(1)}, bf16[2048,512]{1,0:T(8,128)(2,1)}, u32[]{:S(2)}) copy-start(bf16[2048,512]{1,0:T(8,128)(2,1)} %features_ref.7) | copy-start | bytes 6291460
  15.1 19.7 %copy-start.1 = (bf16[512,1024]{1,0:T(8,128)(2,1)S(1)}, bf16[512,1024]{1,0:T(8,128)(2,1)}, u32[]{:S(2)}) copy-start(bf16[512,1024]{1,0:T(8,128)(2,1)} %w1_ref.7) | copy-start | bytes 3145732
  15.1 19.7 %copy-start.2 = (bf16[1024,256]{1,0:T(8,128)(2,1)S(1)}, bf16[1024,256]{1,0:T(8,128)(2,1)}, u32[]{:S(2)}) copy-start(bf16[1024,256]{1,0:T(8,128)(2,1)} %w2_ref.7) | copy-start | bytes 1572868
  15.2 10.6 %collective-permute-start.2 = (f32[256,128]{1,0:T(8,128)S(1)}, f32[256,128]{1,0:T(8,128)S(1)}, u32[]{:S(2)}, u32[]{:S(2)}) collective-permute-start(f32[256,128]{1,0:T(8,128)S(1)} %pool.6.after_ref), channel_id=1, source_target_pairs={{0,4},{4,8},{8,12},{12,0},{1,5},{5,9},{9,13},{13,1},{2,6},{6,10},{... | collective-permute-start | bytes 393224 | tf_op jit(solution)/shard_map/ppermute | solution.py:338
  18.3 11.2 %collective-permute-start.1 = (f32[256,128]{1,0:T(8,128)S(1)}, f32[256,128]{1,0:T(8,128)S(1)}, u32[]{:S(2)}, u32[]{:S(2)}) collective-permute-start(f32[256,128]{1,0:T(8,128)S(1)} %pool.5.after_ref), channel_id=1, source_target_pairs={{0,8},{4,12},{8,0},{12,4},{1,9},{5,13},{9,1},{13,5},{2,10},{6,14},... | collective-permute-start | bytes 393224 | tf_op jit(solution)/shard_map/ppermute | solution.py:338
  20.8 8.6 %collective-permute-start = (f32[256,128]{1,0:T(8,128)S(1)}, f32[256,128]{1,0:T(8,128)S(1)}, u32[]{:S(2)}, u32[]{:S(2)}) collective-permute-start(f32[256,128]{1,0:T(8,128)S(1)} %pool.4.after_ref), channel_id=1, source_target_pairs={{0,12},{4,0},{8,4},{12,8},{1,13},{5,1},{9,5},{13,9},{2,14},{6,2},{... | collective-permute-start | bytes 393224 | tf_op jit(solution)/shard_map/ppermute | solution.py:338
  29.9 1.4 %collective-permute-start.3 = (f32[128,256]{1,0:T(8,128)S(1)}, f32[128,256]{1,0:T(8,128)S(1)}, u32[]{:S(2)}, u32[]{:S(2)}) collective-permute-start(f32[128,256]{1,0:T(8,128)S(1)} %project.2.refs_5_.after_ref), channel_id=1, source_target_pairs={{0,1},{1,0},{2,3},{3,2},{4,5},{5,4},{6,7},{7,6},{8,9},{9,8},{10,11... | collective-permute-start | bytes 393224 | tf_op jit(solution)/shard_map/ppermute | solution.py:327
  30.3 13.0 %copy-start.5 = (s32[2048]{0:T(1024)S(1)}, s32[2048]{0:T(1024)}, u32[]{:S(2)}) copy-start(s32[2048]{0:T(1024)} %param.15) | copy-start | bytes 24580
  31.3 7.3 %collective-permute-start.6 = (f32[128,256]{1,0:T(8,128)S(1)}, f32[128,256]{1,0:T(8,128)S(1)}, u32[]{:S(2)}, u32[]{:S(2)}) collective-permute-start(f32[128,256]{1,0:T(8,128)S(1)} %add.12), channel_id=1, source_target_pairs={{0,18},{1,19},{2,16},{3,17},{16,2},{17,3},{18,0},{19,1},{4,22},{5,... | collective-permute-start | bytes 393224 | tf_op jit(solution)/shard_map/ppermute | solution.py:333
  33.8 6.9 %collective-permute-start.5 = (f32[128,256]{1,0:T(8,128)S(1)}, f32[128,256]{1,0:T(8,128)S(1)}, u32[]{:S(2)}, u32[]{:S(2)}) collective-permute-start(f32[128,256]{1,0:T(8,128)S(1)} %add.12), channel_id=1, source_target_pairs={{0,16},{1,17},{2,18},{3,19},{16,0},{17,1},{18,2},{19,3},{4,20},{5,... | collective-permute-start | bytes 393224 | tf_op jit(solution)/shard_map/ppermute | solution.py:333
  34.3 6.3 %collective-permute-start.4 = (f32[128,256]{1,0:T(8,128)S(1)}, f32[128,256]{1,0:T(8,128)S(1)}, u32[]{:S(2)}, u32[]{:S(2)}) collective-permute-start(f32[128,256]{1,0:T(8,128)S(1)} %add.12), channel_id=1, source_target_pairs={{0,2},{1,3},{2,0},{3,1},{16,18},{17,19},{18,16},{19,17},{4,6},{5,7... | collective-permute-start | bytes 393224 | tf_op jit(solution)/shard_map/ppermute | solution.py:333
  40.7 3.8 %collective-permute-start.7 = (f32[128,256]{1,0:T(8,128)S(1)}, f32[128,256]{1,0:T(8,128)S(1)}, u32[]{:S(2)}, u32[]{:S(2)}) collective-permute-start(f32[128,256]{1,0:T(8,128)S(1)} %add_add_fusion.mine_ref.refs_9_), channel_id=1, source_target_pairs={{0,1},{1,0},{2,3},{3,2},{4,5},{5,4},{6,7},{7,6},{8,9},{9,8},{10,11... | collective-permute-start | bytes 393224 | tf_op jit(solution)/shard_map/ppermute | solution.py:327
  45.8 6.1 %collective-permute-start.10 = (f32[2,2048]{1,0:T(2,128)S(1)}, f32[2,2048]{1,0:T(2,128)S(1)}, u32[]{:S(2)}, u32[]{:S(2)}) collective-permute-start(f32[2,2048]{1,0:T(2,128)S(1)} %get-tuple-element.25.refs_0_), channel_id=1, source_target_pairs={{0,12},{4,8},{8,4},{12,0},{1,13},{5,9},{9,5},{13,1},{2,14},{6,10},... | collective-permute-start | bytes 49160 | tf_op jit(solution)/shard_map/ppermute | solution.py:327
  50.2 4.6 %collective-permute-start.9 = (f32[2,2048]{1,0:T(2,128)S(1)}, f32[2,2048]{1,0:T(2,128)S(1)}, u32[]{:S(2)}, u32[]{:S(2)}) collective-permute-start(f32[2,2048]{1,0:T(2,128)S(1)} %get-tuple-element.25.refs_0_), channel_id=1, source_target_pairs={{0,8},{4,12},{8,0},{12,4},{1,9},{5,13},{9,1},{13,5},{2,10},{6,14},... | collective-permute-start | bytes 49160 | tf_op jit(solution)/shard_map/ppermute | solution.py:327
  50.6 4.2 %collective-permute-start.8 = (f32[2,2048]{1,0:T(2,128)S(1)}, f32[2,2048]{1,0:T(2,128)S(1)}, u32[]{:S(2)}, u32[]{:S(2)}) collective-permute-start(f32[2,2048]{1,0:T(2,128)S(1)} %get-tuple-element.25.refs_0_), channel_id=1, source_target_pairs={{0,4},{4,0},{8,12},{12,8},{1,5},{5,1},{9,13},{13,9},{2,6},{6,2},{1... | collective-permute-start | bytes 49160 | tf_op jit(solution)/shard_map/ppermute | solution.py:327
